TPU v7x, 512 devices: a whole 4x8x8 slice. The times are simulated.
512 devices in a mesh: grp: 16 (over y, x_lo), row: 8 (over z), col: 4 (over x_hi, core).
Axes of the slice: x: 4 (x_hi: 2, x_lo: 2; x = x_hi * 2 + x_lo), y: 8, z: 8, core: 2. Of those that a mesh axis runs over, the one named last changes fastest.
Arguments:
- normals: float32 [16, 4096, 4096], P('grp', 'row', 'col'), as said below
- transforms: float32 [16, 32, 128, 128], P('grp', 'row'), as said below
- block_map: int32 [16, 32], P('grp'), may hold values from 0 to 31, as said below
Outputs:
- eliminated: float32 [4096, 4096], P('row', 'col')
Inputs may be any that keep to these rules, and one draw needn't show every extreme that they name: `block_map`: for each group, a permutation of the blocks that maps every aligned range of 4 blocks onto itself. `normals`: each group's matrix is symmetric positive definite. `transforms`: each block is nonsingular.
All inputs are finite; a program needn't handle non-finite values.
Results may differ from a plain program's by a relative error of at most 0.0001.
Values sent between devices are 32-bit elements; how exact they have to be, the bound alone decides.
A program may use at most 64 MiB of HBM per device.

v0:
```python
import jax
import jax.numpy as jnp
from jax import lax
from jax.sharding import PartitionSpec as P

BLK = 128
NPAN = 5


def split_up(shard, dim, length):
    shape = shard.shape
    parts = shard.reshape(*shape[:dim], length, shape[dim] // length, *shape[dim + 1 :])
    return jnp.moveaxis(parts, dim, 0)


def sum_at_owner(shard, axis, dim):
    parts = split_up(shard, dim, lax.axis_size(axis))
    arrived = lax.all_to_all(parts, axis, split_axis=0, concat_axis=0, tiled=True)
    return arrived.sum(axis=0)


def from_root(shard, axis, root):
    return lax.dynamic_index_in_dim(lax.all_gather(shard, axis), root, 0, keepdims=False)


def in_order(parts, dim):
    parts = jnp.moveaxis(parts, 0, dim)
    shape = parts.shape
    return parts.reshape(*shape[:dim], shape[dim] * shape[dim + 1], *shape[dim + 2 :])


def sent_to_all(shard, axis):
    length = lax.axis_size(axis)
    return lax.all_to_all(
        jnp.broadcast_to(shard[None], (length, *shard.shape)), axis, 0, 0, tiled=True
    )


def gather_directly(shard, axis, dim):
    return in_order(sent_to_all(shard, axis), dim)


def on_device(normals, transforms, block_map):
    local = normals[0]
    height, width = local.shape
    row_blocks = height // BLK
    col_blocks = width // BLK
    row_index = lax.axis_index("row")
    col_index = lax.axis_index("col")
    row_transforms = transforms[0]
    every_block = lax.all_gather(transforms, "row", axis=1, tiled=True)[0]
    col_transforms = lax.dynamic_slice_in_dim(every_block, col_index * col_blocks, col_blocks, 0)
    grid = local.reshape(row_blocks, BLK, col_blocks, BLK)
    half_done = jnp.einsum("aij,aibk->ajbk", row_transforms, grid, precision=lax.Precision.HIGHEST)
    rotated = jnp.einsum(
        "ajbk,bkl->ajbl", half_done, col_transforms, precision=lax.Precision.HIGHEST
    )
    mapping = block_map[0]
    row_map = (
        lax.dynamic_slice_in_dim(mapping, row_index * row_blocks, row_blocks, 0)
        - row_index * row_blocks
    )
    col_map = (
        lax.dynamic_slice_in_dim(mapping, col_index * col_blocks, col_blocks, 0)
        - col_index * col_blocks
    )
    rotated = jnp.take(rotated, row_map, axis=0)
    rotated = jnp.take(rotated, col_map, axis=2).reshape(height, width)
    matrix = sum_at_owner(rotated, "grp", 0)
    row_offset = row_index * height + lax.axis_index("grp") * matrix.shape[0]
    own_count = matrix.shape[0]
    order_all = height * lax.axis_size("row")
    col_offset = col_index * width
    for panel in range(NPAN):
        offset = panel * BLK
        holder = offset // width
        inside = offset - holder * width
        panel_piece = from_root(matrix[:, inside : inside + BLK], "col", holder)
        panel_piece = gather_directly(panel_piece, "grp", 0)
        column = lax.all_gather(panel_piece, "row", axis=0, tiled=True)
        factor_block = jnp.linalg.cholesky(column[offset : offset + BLK])
        factor = lax.linalg.triangular_solve(
            factor_block, column, left_side=False, lower=True, transpose_a=True
        )
        below = jnp.arange(order_all)[:, None] >= offset
        factor = jnp.where(below, factor, jnp.zeros_like(factor))
        own_rows = lax.dynamic_slice_in_dim(factor, row_offset, own_count, 0)
        col_rows = lax.dynamic_slice_in_dim(factor, col_offset, width, 0)
        matrix = matrix - jnp.dot(
            own_rows,
            col_rows.T,
            precision=lax.Precision.HIGHEST,
            preferred_element_type=jnp.float32,
        )
        current = matrix[:, inside : inside + BLK]
        matrix = matrix.at[:, inside : inside + BLK].set(
            jnp.where(col_index == holder, own_rows, current)
        )
    matrix = gather_directly(matrix, "grp", 0)
    return matrix


def solution(mesh):
    return jax.shard_map(
        on_device,
        mesh=mesh,
        in_specs=(P("grp", "row", "col"), P("grp", "row", None, None), P("grp", None)),
        out_specs=P("row", "col"),
        check_vma=False,
    )
```

profile of v0, /device:TPU:4, one launch (start us, length us, event | category | flops | bytes accessed | tf_op | source)
XLA Modules:
  0.0 668.6 jit_solution(9049926611283162796)
XLA Ops:
  14.9 43.2 %all-gather.12.cloned.1.call-done = f32[1,32,128,128]{3,2,0,1:T(8,128)} async-done(((f32[1,4,128,128]{3,2,0,1:T(8,128)}), f32[1,32,128,128]{3,2,0,1:T(8,128)}) %all-gather.12.cloned.1.call-update) | async-done | bytes 2097168 | tf_op jit(solution)/shard_map/all_gather | solution.py:51
  72.3 54.1 %all_to_all.35 = f32[16,32,1024]{2,1,0:T(8,128)S(1)} all-to-all(f32[16,32,1024]{2,1,0:T(8,128)S(1)} %broadcast_select_fusion), channel_id=1, replica_groups=mesh['grp'=16,'row'=8,'col'=4] {'grp'}, dimensions={0} | all-to-all | bytes 4194304 | tf_op jit(solution)/shard_map/all_to_all | solution.py:18
  133.3 15.9 %all_to_all.36 = f32[16,32,128]{2,1,0:T(8,128)S(1)} all-to-all(f32[16,32,128]{2,1,0:T(8,128)S(1)} %broadcast_in_dim.111), channel_id=1, replica_groups=mesh['grp'=16,'row'=8,'col'=4] {'grp'}, dimensions={0} | all-to-all | bytes 524288 | tf_op jit(solution)/shard_map/all_to_all | solution.py:34
  150.9 36.5 %all-gather.14.cloned.1.call-done = f32[4096,128]{0,1:T(8,128)} async-done(((f32[512,128]{0,1:T(8,128)}), f32[4096,128]{0,1:T(8,128)}) %all-gather.14.cloned.1.call-update) | async-done | bytes 2097168 | tf_op jit(solution)/shard_map/all_gather | solution.py:80
  189.1 11.7 %cholesky.89 = f32[128,128]{1,0:T(8,128)S(1)} custom-call(f32[128,128]{1,0:T(8,128)S(1)} %fusion.28), custom_call_target="Cholesky" | custom-call | tf_op jit(solution)/shard_map/jit(cholesky)/cholesky | solution.py:81
  202.2 9.8 %custom-call.9 = f32[1,128,128]{1,2,0:T(8,128)S(1)} custom-call(f32[1,128,128]{2,1,0:T(8,128)S(1)} %fusion.14), custom_call_target="InvertDiagBlocksLowerTriangular" | custom-call | tf_op jit(solution)/shard_map/triangular_solve/custom-call.0 | solution.py:82
  218.4 6.7 %all-gather.1 = f32[128,128]{1,0:T(8,128)S(1)} all-gather(f32[32,128]{1,0:T(8,128)S(1)} %slice.169), channel_id=3, replica_groups=mesh['grp'=16,'row'=8,'col'=4] {'col'}, dimensions={0}, use_global_device_ids=true | all-gather | bytes 81920 | tf_op jit(solution)/shard_map/all_gather | solution.py:23
  225.2 19.7 %all_to_all.37 = f32[16,32,128]{2,1,0:T(8,128)S(1)} all-to-all(f32[16,32,128]{2,1,0:T(8,128)S(1)} %broadcast_in_dim.114), channel_id=1, replica_groups=mesh['grp'=16,'row'=8,'col'=4] {'grp'}, dimensions={0} | all-to-all | bytes 524288 | tf_op jit(solution)/shard_map/all_to_all | solution.py:34
  246.7 37.3 %all-gather.16.cloned.1.call-done = f32[4096,128]{0,1:T(8,128)} async-done(((f32[512,128]{0,1:T(8,128)}), f32[4096,128]{0,1:T(8,128)}) %all-gather.16.cloned.1.call-update) | async-done | bytes 2097168 | tf_op jit(solution)/shard_map/all_gather | solution.py:80
  285.8 11.7 %cholesky.100 = f32[128,128]{1,0:T(8,128)S(1)} custom-call(f32[128,128]{1,0:T(8,128)S(1)} %fusion.26), custom_call_target="Cholesky" | custom-call | tf_op jit(solution)/shard_map/jit(cholesky)/cholesky | solution.py:81
  298.8 9.8 %custom-call.10 = f32[1,128,128]{1,2,0:T(8,128)S(1)} custom-call(f32[1,128,128]{2,1,0:T(8,128)S(1)} %fusion.15), custom_call_target="InvertDiagBlocksLowerTriangular" | custom-call | tf_op jit(solution)/shard_map/triangular_solve/custom-call.0 | solution.py:82
  322.0 19.7 %all_to_all.38 = f32[16,32,128]{2,1,0:T(8,128)S(1)} all-to-all(f32[16,32,128]{2,1,0:T(8,128)S(1)} %broadcast_in_dim.117), channel_id=1, replica_groups=mesh['grp'=16,'row'=8,'col'=4] {'grp'}, dimensions={0} | all-to-all | bytes 524288 | tf_op jit(solution)/shard_map/all_to_all | solution.py:34
  343.7 37.1 %all-gather.18.cloned.1.call-done = f32[4096,128]{0,1:T(8,128)} async-done(((f32[512,128]{0,1:T(8,128)}), f32[4096,128]{0,1:T(8,128)}) %all-gather.18.cloned.1.call-update) | async-done | bytes 2097168 | tf_op jit(solution)/shard_map/all_gather | solution.py:80
  382.6 11.7 %cholesky.111 = f32[128,128]{1,0:T(8,128)S(1)} custom-call(f32[128,128]{1,0:T(8,128)S(1)} %fusion.24), custom_call_target="Cholesky" | custom-call | tf_op jit(solution)/shard_map/jit(cholesky)/cholesky | solution.py:81
  395.7 9.8 %custom-call.11 = f32[1,128,128]{1,2,0:T(8,128)S(1)} custom-call(f32[1,128,128]{2,1,0:T(8,128)S(1)} %fusion.16), custom_call_target="InvertDiagBlocksLowerTriangular" | custom-call | tf_op jit(solution)/shard_map/triangular_solve/custom-call.0 | solution.py:82
  418.8 19.7 %all_to_all.39 = f32[16,32,128]{2,1,0:T(8,128)S(1)} all-to-all(f32[16,32,128]{2,1,0:T(8,128)S(1)} %broadcast_in_dim.120), channel_id=1, replica_groups=mesh['grp'=16,'row'=8,'col'=4] {'grp'}, dimensions={0} | all-to-all | bytes 524288 | tf_op jit(solution)/shard_map/all_to_all | solution.py:34
  440.2 37.4 %all-gather.20.cloned.1.call-done = f32[4096,128]{0,1:T(8,128)} async-done(((f32[512,128]{0,1:T(8,128)}), f32[4096,128]{0,1:T(8,128)}) %all-gather.20.cloned.1.call-update) | async-done | bytes 2097168 | tf_op jit(solution)/shard_map/all_gather | solution.py:80
  479.4 11.7 %cholesky.122 = f32[128,128]{1,0:T(8,128)S(1)} custom-call(f32[128,128]{1,0:T(8,128)S(1)} %fusion.22), custom_call_target="Cholesky" | custom-call | tf_op jit(solution)/shard_map/jit(cholesky)/cholesky | solution.py:81
  492.5 9.8 %custom-call.12 = f32[1,128,128]{1,2,0:T(8,128)S(1)} custom-call(f32[1,128,128]{2,1,0:T(8,128)S(1)} %fusion.17), custom_call_target="InvertDiagBlocksLowerTriangular" | custom-call | tf_op jit(solution)/shard_map/triangular_solve/custom-call.0 | solution.py:82
  515.6 19.9 %all_to_all.40 = f32[16,32,128]{2,1,0:T(8,128)S(1)} all-to-all(f32[16,32,128]{2,1,0:T(8,128)S(1)} %broadcast_in_dim.123), channel_id=1, replica_groups=mesh['grp'=16,'row'=8,'col'=4] {'grp'}, dimensions={0} | all-to-all | bytes 524288 | tf_op jit(solution)/shard_map/all_to_all | solution.py:34
  537.0 37.6 %all-gather.22.cloned.1.call-done = f32[4096,128]{0,1:T(8,128)} async-done(((f32[512,128]{0,1:T(8,128)}), f32[4096,128]{0,1:T(8,128)}) %all-gather.22.cloned.1.call-update) | async-done | bytes 2097168 | tf_op jit(solution)/shard_map/all_gather | solution.py:80
  576.5 11.7 %cholesky.133 = f32[128,128]{1,0:T(8,128)S(1)} custom-call(f32[128,128]{1,0:T(8,128)S(1)} %fusion.20), custom_call_target="Cholesky" | custom-call | tf_op jit(solution)/shard_map/jit(cholesky)/cholesky | solution.py:81
  589.5 9.8 %custom-call.13 = f32[1,128,128]{1,2,0:T(8,128)S(1)} custom-call(f32[1,128,128]{2,1,0:T(8,128)S(1)} %fusion.18), custom_call_target="InvertDiagBlocksLowerTriangular" | custom-call | tf_op jit(solution)/shard_map/triangular_solve/custom-call.0 | solution.py:82
  606.1 54.1 %all_to_all.41 = f32[16,32,1024]{2,1,0:T(8,128)S(1)} all-to-all(f32[16,32,1024]{2,1,0:T(8,128)S(1)} %broadcast_in_dim.125), channel_id=1, replica_groups=mesh['grp'=16,'row'=8,'col'=4] {'grp'}, dimensions={0} | all-to-all | bytes 4194304 | tf_op jit(solution)/shard_map/all_to_all | solution.py:34
  (113 shorter events, 107.9 us)
Async XLA Ops:
  6.5 51.5 %all-gather.12.cloned.1.call-start = ((), (), s32[]{:S(2)}) async-start(), calls=%async_computation.7 | async-start | bytes 2359296 | tf_op jit(solution)/shard_map/all_gather | solution.py:51
  7.3 180.1 %all-gather.14.cloned.1.call-start = ((), (), s32[]{:S(2)}) async-start(), calls=%async_computation.8 | async-start | bytes 2359296 | tf_op jit(solution)/shard_map/all_gather | solution.py:80
  7.3 3.4 copy-start.1
  7.3 3.8 copy-start
  150.0 134.0 %all-gather.16.cloned.1.call-start = ((), (), s32[]{:S(2)}) async-start(), calls=%async_computation.9 | async-start | bytes 2359296 | tf_op jit(solution)/shard_map/all_gather | solution.py:80
  245.7 135.1 %all-gather.18.cloned.1.call-start = ((), (), s32[]{:S(2)}) async-start(), calls=%async_computation.10 | async-start | bytes 2359296 | tf_op jit(solution)/shard_map/all_gather | solution.py:80
  342.6 135.1 %all-gather.20.cloned.1.call-start = ((), (), s32[]{:S(2)}) async-start(), calls=%async_computation.11 | async-start | bytes 2359296 | tf_op jit(solution)/shard_map/all_gather | solution.py:80
  439.4 135.3 %all-gather.22.cloned.1.call-start = ((), (), s32[]{:S(2)}) async-start(), calls=%async_computation.12 | async-start | bytes 2359296 | tf_op jit(solution)/shard_map/all_gather | solution.py:80
Sparse Core Ops, SparseCore 0:
  9.4 48.5 all-gather.11
  150.1 37.1 all-gather.13
  245.9 38.0 all-gather.15
  342.7 38.0 all-gather.17
  439.5 38.0 all-gather.19
  536.5 38.1 all-gather.21
where the time goes:
time: 675 us; the launch traced here: 669 us
  blocking collectives  237 us (35%)
  waiting for transfers between devices  230 us (34%)
  other arithmetic  127 us (19%)
  matrix products  37.3 us (6%)
  local copies, waits for them, and re-layouts  22.1 us (3%)
  between operations  14.2 us (2%)
    all_gather x5, waiting for transfers between devices, on_device(): column = lax.all_gather(panel_piece, 'row', axis=0, tiled=True)  186 us
    all_to_all x6, blocking collectives, sent_to_all(): lax.all_to_all(jnp.broadcast_to(shard[None], (length, *shard.shape)), axi...  149 us
    another operation x15, other arithmetic, on_device(): factor_block = jnp.linalg.cholesky(column[offset:offset + BLK])  61.9 us
    all_to_all x1, blocking collectives, sum_at_owner(): lax.all_to_all(parts, axis, split_axis=0, concat_axis=0, tiled=True)  54.1 us
    another operation x10, other arithmetic, on_device(): lax.linalg.triangular_solve(factor_block, column, left_side=False, lower=...  52.3 us
    all_gather x1, waiting for transfers between devices, on_device(): every_block = lax.all_gather(transforms, 'row', axis=1, tiled=True)[0]  43.2 us
    all_gather x5, blocking collectives, from_root(): lax.all_gather(shard, axis)  33.7 us
    another operation x5, matrix products, on_device(): lax.linalg.triangular_solve(factor_block, column, left_side=False, lower=...  26.2 us
  transfers between devices with their start and end apart: 6, of which 6 were waited for; matrix products, arithmetic and copies ran while one was open for 2% of the time, Pallas kernels for 0%

commit v1 on v0

--- a/solution.py
+++ b/solution.py
@@ -77,7 +77,14 @@
         inside = offset - holder * width
         panel_piece = from_root(matrix[:, inside : inside + BLK], "col", holder)
         panel_piece = gather_directly(panel_piece, "grp", 0)
-        column = lax.all_gather(panel_piece, "row", axis=0, tiled=True)
+        cores_n = lax.axis_size("row")
+        column = lax.all_to_all(
+            jnp.tile(panel_piece, [cores_n if num == 0 else 1 for num in range(panel_piece.ndim)]),
+            "row",
+            split_axis=0,
+            concat_axis=0,
+            tiled=True,
+        )
         factor_block = jnp.linalg.cholesky(column[offset : offset + BLK])
         factor = lax.linalg.triangular_solve(
             factor_block, column, left_side=False, lower=True, transpose_a=True

time: 675 us -> 747 us (1.11)
  waiting for transfers between devices: 230 us -> 292 us
  starting transfers between devices: 1.17 us -> 19.7 us
  local copies, waits for them, and re-layouts: 22.1 us -> 38 us
  blocking collectives: 237 us -> 222 us
    all_to_all x0 -> x5, waiting for transfers between devices: none -> 248 us  [on_device(): lax.all_to_all(jnp.tile(panel_piece, [cores_n if num == 0 else 1 for num...]
    all_gather x5 -> x0, waiting for transfers between devices: 186 us -> none  [on_device(): column = lax.all_gather(panel_piece, 'row', axis=0, tiled=True)]
    all_to_all x0 -> x5, starting transfers between devices: none -> 19.7 us  [on_device(): lax.all_to_all(jnp.tile(panel_piece, [cores_n if num == 0 else 1 for num...]
    all_to_all x6, blocking collectives: 149 us -> 134 us  [sent_to_all(): lax.all_to_all(jnp.broadcast_to(shard[None], (length, *shard.shape)), axi...]
    all_to_all x0 -> x5, local copies, waits for them, and re-layouts: none -> 9.11 us  [on_device(): lax.all_to_all(jnp.tile(panel_piece, [cores_n if num == 0 else 1 for num...]
    another operation x0 -> x10, local copies, waits for them, and re-layouts: none -> 8.56 us  [on_device(): jnp.tile(panel_piece, [cores_n if num == 0 else 1 for num in range(panel_...]
where the time goes in v1:
time: 747 us; the launch traced here: 740 us
  waiting for transfers between devices  292 us (39%)
  blocking collectives  222 us (30%)
  other arithmetic  124 us (17%)
  local copies, waits for them, and re-layouts  38 us (5%)
  matrix products  30.8 us (4%)
  starting transfers between devices  19.7 us (3%)
  between operations  14.5 us (2%)
    all_to_all x5, waiting for transfers between devices, on_device(): lax.all_to_all(jnp.tile(panel_piece, [cores_n if num == 0 else 1 for num...  248 us
    all_to_all x6, blocking collectives, sent_to_all(): lax.all_to_all(jnp.broadcast_to(shard[None], (length, *shard.shape)), axi...  134 us
    another operation x15, other arithmetic, on_device(): factor_block = jnp.linalg.cholesky(column[offset:offset + BLK])  61.9 us
    all_to_all x1, blocking collectives, sum_at_owner(): lax.all_to_all(parts, axis, split_axis=0, concat_axis=0, tiled=True)  54.1 us
    another operation x10, other arithmetic, on_device(): lax.linalg.triangular_solve(factor_block, column, left_side=False, lower=...  52.3 us
    all_gather x1, waiting for transfers between devices, on_device(): every_block = lax.all_gather(transforms, 'row', axis=1, tiled=True)[0]  43.2 us
    all_gather x5, blocking collectives, from_root(): lax.all_gather(shard, axis)  33.7 us
    another operation x5, matrix products, on_device(): lax.linalg.triangular_solve(factor_block, column, left_side=False, lower=...  19.7 us
  transfers between devices with their start and end apart: 6, of which 6 were waited for; matrix products, arithmetic and copies ran while one was open for 2% of the time, Pallas kernels for 0%

profile of v1, /device:TPU:4, one launch (start us, length us, event | category | flops | bytes accessed | tf_op | source)
XLA Modules:
  0.0 740.1 jit_solution(13373262915643850274)
XLA Ops:
  14.8 43.2 %all-gather.7.cloned.1.call-done = f32[1,32,128,128]{3,2,0,1:T(8,128)} async-done(((f32[1,4,128,128]{3,2,0,1:T(8,128)}), f32[1,32,128,128]{3,2,0,1:T(8,128)}) %all-gather.7.cloned.1.call-update) | async-done | bytes 2097168 | tf_op jit(solution)/shard_map/all_gather | solution.py:51
  72.3 54.1 %all_to_all.80 = f32[16,32,1024]{2,1,0:T(8,128)S(1)} all-to-all(f32[16,32,1024]{2,1,0:T(8,128)S(1)} %broadcast_select_fusion), channel_id=1, replica_groups=mesh['grp'=16,'row'=8,'col'=4] {'grp'}, dimensions={0} | all-to-all | bytes 4194304 | tf_op jit(solution)/shard_map/all_to_all | solution.py:18
  133.3 15.9 %all_to_all.81 = f32[16,32,128]{2,1,0:T(8,128)S(1)} all-to-all(f32[16,32,128]{2,1,0:T(8,128)S(1)} %broadcast_in_dim.111), channel_id=1, replica_groups=mesh['grp'=16,'row'=8,'col'=4] {'grp'}, dimensions={0} | all-to-all | bytes 524288 | tf_op jit(solution)/shard_map/all_to_all | solution.py:34
  155.8 49.0 %all-to-all-done.2 = f32[8,512,128]{1,2,0:T(8,128)S(1)} async-done(((f32[8,512,128]{1,2,0:T(8,128)}), f32[8,512,128]{1,2,0:T(8,128)S(1)}, u32[]{:S(2)}, u32[]{:S(2)}) %all-to-all-start.2) | async-done | bytes 2097184 | tf_op jit(solution)/shard_map/all_to_all | solution.py:81
  208.1 11.7 %cholesky.89 = f32[128,128]{1,0:T(8,128)S(1)} custom-call(f32[128,128]{1,0:T(8,128)S(1)} %fusion.28), custom_call_target="Cholesky" | custom-call | tf_op jit(solution)/shard_map/jit(cholesky)/cholesky | solution.py:88
  221.1 9.8 %custom-call.9 = f32[1,128,128]{1,2,0:T(8,128)S(1)} custom-call(f32[1,128,128]{2,1,0:T(8,128)S(1)} %fusion.14), custom_call_target="InvertDiagBlocksLowerTriangular" | custom-call | tf_op jit(solution)/shard_map/triangular_solve/custom-call.0 | solution.py:89
  235.8 6.7 all-gather.1
  242.6 16.0 %all_to_all.82 = f32[16,32,128]{2,1,0:T(8,128)S(1)} all-to-all(f32[16,32,128]{2,1,0:T(8,128)S(1)} %broadcast_in_dim.114), channel_id=1, replica_groups=mesh['grp'=16,'row'=8,'col'=4] {'grp'}, dimensions={0} | all-to-all | bytes 524288 | tf_op jit(solution)/shard_map/all_to_all | solution.py:34
  265.0 49.8 %all-to-all-done.4 = f32[8,512,128]{1,2,0:T(8,128)S(1)} async-done(((f32[8,512,128]{1,2,0:T(8,128)}), f32[8,512,128]{1,2,0:T(8,128)S(1)}, u32[]{:S(2)}, u32[]{:S(2)}) %all-to-all-start.4) | async-done | bytes 2097184 | tf_op jit(solution)/shard_map/all_to_all | solution.py:81
  318.1 11.7 %cholesky.100 = f32[128,128]{1,0:T(8,128)S(1)} custom-call(f32[128,128]{1,0:T(8,128)S(1)} %fusion.26), custom_call_target="Cholesky" | custom-call | tf_op jit(solution)/shard_map/jit(cholesky)/cholesky | solution.py:88
  331.1 9.8 %custom-call.10 = f32[1,128,128]{1,2,0:T(8,128)S(1)} custom-call(f32[1,128,128]{2,1,0:T(8,128)S(1)} %fusion.15), custom_call_target="InvertDiagBlocksLowerTriangular" | custom-call | tf_op jit(solution)/shard_map/triangular_solve/custom-call.0 | solution.py:89
  353.1 15.7 %all_to_all.83 = f32[16,32,128]{2,1,0:T(8,128)S(1)} all-to-all(f32[16,32,128]{2,1,0:T(8,128)S(1)} %broadcast_in_dim.117), channel_id=1, replica_groups=mesh['grp'=16,'row'=8,'col'=4] {'grp'}, dimensions={0} | all-to-all | bytes 524288 | tf_op jit(solution)/shard_map/all_to_all | solution.py:34
  375.1 49.8 %all-to-all-done.6 = f32[8,512,128]{1,2,0:T(8,128)S(1)} async-done(((f32[8,512,128]{1,2,0:T(8,128)}), f32[8,512,128]{1,2,0:T(8,128)S(1)}, u32[]{:S(2)}, u32[]{:S(2)}) %all-to-all-start.6) | async-done | bytes 2097184 | tf_op jit(solution)/shard_map/all_to_all | solution.py:81
  428.1 11.7 %cholesky.111 = f32[128,128]{1,0:T(8,128)S(1)} custom-call(f32[128,128]{1,0:T(8,128)S(1)} %fusion.24), custom_call_target="Cholesky" | custom-call | tf_op jit(solution)/shard_map/jit(cholesky)/cholesky | solution.py:88
  441.2 9.8 %custom-call.11 = f32[1,128,128]{1,2,0:T(8,128)S(1)} custom-call(f32[1,128,128]{2,1,0:T(8,128)S(1)} %fusion.16), custom_call_target="InvertDiagBlocksLowerTriangular" | custom-call | tf_op jit(solution)/shard_map/triangular_solve/custom-call.0 | solution.py:89
  463.1 15.7 %all_to_all.84 = f32[16,32,128]{2,1,0:T(8,128)S(1)} all-to-all(f32[16,32,128]{2,1,0:T(8,128)S(1)} %broadcast_in_dim.120), channel_id=1, replica_groups=mesh['grp'=16,'row'=8,'col'=4] {'grp'}, dimensions={0} | all-to-all | bytes 524288 | tf_op jit(solution)/shard_map/all_to_all | solution.py:34
  485.1 49.8 %all-to-all-done.8 = f32[8,512,128]{1,2,0:T(8,128)S(1)} async-done(((f32[8,512,128]{1,2,0:T(8,128)}), f32[8,512,128]{1,2,0:T(8,128)S(1)}, u32[]{:S(2)}, u32[]{:S(2)}) %all-to-all-start.8) | async-done | bytes 2097184 | tf_op jit(solution)/shard_map/all_to_all | solution.py:81
  538.2 11.7 %cholesky.122 = f32[128,128]{1,0:T(8,128)S(1)} custom-call(f32[128,128]{1,0:T(8,128)S(1)} %fusion.22), custom_call_target="Cholesky" | custom-call | tf_op jit(solution)/shard_map/jit(cholesky)/cholesky | solution.py:88
  551.2 9.8 %custom-call.12 = f32[1,128,128]{1,2,0:T(8,128)S(1)} custom-call(f32[1,128,128]{2,1,0:T(8,128)S(1)} %fusion.17), custom_call_target="InvertDiagBlocksLowerTriangular" | custom-call | tf_op jit(solution)/shard_map/triangular_solve/custom-call.0 | solution.py:89
  573.2 15.7 %all_to_all.85 = f32[16,32,128]{2,1,0:T(8,128)S(1)} all-to-all(f32[16,32,128]{2,1,0:T(8,128)S(1)} %broadcast_in_dim.123), channel_id=1, replica_groups=mesh['grp'=16,'row'=8,'col'=4] {'grp'}, dimensions={0} | all-to-all | bytes 524288 | tf_op jit(solution)/shard_map/all_to_all | solution.py:34
  595.3 49.8 %all-to-all-done.10 = f32[8,512,128]{1,2,0:T(8,128)S(1)} async-done(((f32[8,512,128]{1,2,0:T(8,128)}), f32[8,512,128]{1,2,0:T(8,128)S(1)}, u32[]{:S(2)}, u32[]{:S(2)}) %all-to-all-start.10) | async-done | bytes 2097184 | tf_op jit(solution)/shard_map/all_to_all | solution.py:81
  648.3 11.7 %cholesky.133 = f32[128,128]{1,0:T(8,128)S(1)} custom-call(f32[128,128]{1,0:T(8,128)S(1)} %fusion.20), custom_call_target="Cholesky" | custom-call | tf_op jit(solution)/shard_map/jit(cholesky)/cholesky | solution.py:88
  661.4 9.8 %custom-call.13 = f32[1,128,128]{1,2,0:T(8,128)S(1)} custom-call(f32[1,128,128]{2,1,0:T(8,128)S(1)} %fusion.18), custom_call_target="InvertDiagBlocksLowerTriangular" | custom-call | tf_op jit(solution)/shard_map/triangular_solve/custom-call.0 | solution.py:89
  676.8 54.7 %all_to_all.86 = f32[16,32,1024]{2,1,0:T(8,128)S(1)} all-to-all(f32[16,32,1024]{2,1,0:T(8,128)S(1)} %broadcast_in_dim.125), channel_id=1, replica_groups=mesh['grp'=16,'row'=8,'col'=4] {'grp'}, dimensions={0} | all-to-all | bytes 4194304 | tf_op jit(solution)/shard_map/all_to_all | solution.py:34
  (128 shorter events, 132.3 us)
Async XLA Ops:
  6.5 51.5 %all-gather.7.cloned.1.call-start = ((), (), s32[]{:S(2)}) async-start(), calls=%async_computation.12 | async-start | bytes 2359296 | tf_op jit(solution)/shard_map/all_gather | solution.py:51
  7.3 3.4 copy-start.6
  7.3 3.8 copy-start.5
  150.8 53.9 %all-to-all-start.2 = ((f32[8,512,128]{1,2,0:T(8,128)}), f32[8,512,128]{1,2,0:T(8,128)S(1)}, u32[]{:S(2)}, u32[]{:S(2)}) async-start(f32[8,512,128]{1,2,0:T(8,128)} %tile.41), calls=%async_computation.2 | async-start | bytes 4194304 | tf_op jit(solution)/shard_map/all_to_all | solution.py:81
  204.8 1.3 copy-start
  260.3 54.5 %all-to-all-start.4 = ((f32[8,512,128]{1,2,0:T(8,128)}), f32[8,512,128]{1,2,0:T(8,128)S(1)}, u32[]{:S(2)}, u32[]{:S(2)}) async-start(f32[8,512,128]{1,2,0:T(8,128)} %tile.43), calls=%async_computation.4 | async-start | bytes 4194304 | tf_op jit(solution)/shard_map/all_to_all | solution.py:81
  314.8 1.3 copy-start.1
  370.5 54.3 %all-to-all-start.6 = ((f32[8,512,128]{1,2,0:T(8,128)}), f32[8,512,128]{1,2,0:T(8,128)S(1)}, u32[]{:S(2)}, u32[]{:S(2)}) async-start(f32[8,512,128]{1,2,0:T(8,128)} %tile.45), calls=%async_computation.6 | async-start | bytes 4194304 | tf_op jit(solution)/shard_map/all_to_all | solution.py:81
  424.8 1.3 copy-start.2
  480.6 54.3 %all-to-all-start.8 = ((f32[8,512,128]{1,2,0:T(8,128)}), f32[8,512,128]{1,2,0:T(8,128)S(1)}, u32[]{:S(2)}, u32[]{:S(2)}) async-start(f32[8,512,128]{1,2,0:T(8,128)} %tile.47), calls=%async_computation.8 | async-start | bytes 4194304 | tf_op jit(solution)/shard_map/all_to_all | solution.py:81
  534.9 1.3 copy-start.3
  590.7 54.3 %all-to-all-start.10 = ((f32[8,512,128]{1,2,0:T(8,128)}), f32[8,512,128]{1,2,0:T(8,128)S(1)}, u32[]{:S(2)}, u32[]{:S(2)}) async-start(f32[8,512,128]{1,2,0:T(8,128)} %tile.49), calls=%async_computation.10 | async-start | bytes 4194304 | tf_op jit(solution)/shard_map/all_to_all | solution.py:81
  645.0 1.3 copy-start.4
Sparse Core Ops, SparseCore 0:
  9.4 48.5 all-gather.6
